TPU v7x, 768 devices: a whole 4x8x12 slice. The times are simulated.
768 devices in a mesh: gz: 96 (over z, x, core), gy: 8 (over y).
Axes of the slice: x: 4, y: 8, z: 12, core: 2. Of those that a mesh axis runs over, the one named last changes fastest.
Arguments:
- right_side: float32 [768, 64, 256], P('gz', 'gy'), may hold values from -10 to 10, as said below
Outputs:
- solution_field: float32 [768, 64, 256], P('gz', 'gy')
- residual: float32 [768, 64, 256], P('gz', 'gy')
Inputs may be any that keep to these rules, and one draw needn't show every extreme that they name: `right_side`: a right-hand side.
All inputs are finite; a program needn't handle non-finite values.
Results may differ from a plain program's by a relative error of at most 0.00015.
Values sent between devices are 32-bit elements; how exact they have to be, the bound alone decides.
A program may use at most 32 MiB of HBM per device.

v0:
```python
import jax
import jax.numpy as jnp
from jax import lax
from jax.sharding import Mesh
from jax.sharding import PartitionSpec as P

LEVELS = 3
GZ_GY = ("gz_0", "gz_1", "gz_2", "gy")
GZ = ("gz_0", "gz_1", "gz_2")


sweep_order = [
    ((0, 0), (0, 1)),
    ((0, 1), (0, 1)),
    ((1, 0), (0, 1)),
    ((1, 1), (0, 1)),
    ((1, 1), (1, 0)),
    ((1, 0), (1, 0)),
    ((0, 1), (1, 0)),
    ((0, 0), (1, 0)),
]


def extended(block, sides, width):
    for axis, dim in sides:
        count = lax.axis_size(axis)
        forward = [(i, i + 1) for i in range(count - 1)]
        backward = [(target, source) for source, target in forward]
        low = lax.ppermute(
            lax.slice_in_dim(block, block.shape[dim] - width, None, axis=dim), axis, forward
        )
        high = lax.ppermute(lax.slice_in_dim(block, 0, width, axis=dim), axis, backward)
        block = jnp.concatenate([low, block, high], axis=dim)
    return block


def over_axes(value, axes):
    for axis in axes:
        value = lax.psum(value, axis)
    return value


def x_side(field):
    width = [(0, 0)] * (field.ndim - 1)
    upper = jnp.pad(field[..., 1:], width + [(0, 1)])
    lower = jnp.pad(field[..., :-1], width + [(1, 0)])
    return upper + lower


def operate(padded):
    z_cells = padded.shape[0] - 2
    y_cells = padded.shape[1] - 2
    boxed = jnp.zeros((z_cells, y_cells, padded.shape[2]), jnp.float32)
    for z_step in range(3):
        for y_step in range(3):
            boxed = boxed + padded[z_step : z_step + z_cells, y_step : y_step + y_cells, :]
    boxed = boxed + x_side(boxed)
    return 27.0 * padded[1:-1, 1:-1, :] - boxed


def group_update(padded, rhs, z_par, y_par, x_order):
    z_cells = padded.shape[0] - 2
    y_cells = padded.shape[1] - 2
    outer = None
    for z_step in (-1, 0, 1):
        for y_step in (-1, 0, 1):
            if z_step == 0 and y_step == 0:
                continue
            row = padded[
                1 + z_par + z_step : z_cells + z_par + z_step : 2,
                1 + y_par + y_step : y_cells + y_par + y_step : 2,
                :,
            ]
            outer = row if outer is None else outer + row
    center = padded[1 + z_par : z_cells + z_par : 2, 1 + y_par : y_cells + y_par : 2, :]
    total = outer + x_side(outer) + rhs[z_par::2, y_par::2, :]
    parity = jnp.arange(padded.shape[2], dtype=jnp.int32) % 2
    for x_par in x_order:
        center = jnp.where(parity == x_par, (total + x_side(center)) / 26.0, center)
    return padded.at[1 + z_par : z_cells + z_par : 2, 1 + y_par : y_cells + y_par : 2, :].set(
        center
    )


def joint_halo(field):
    return extended(field, ((GZ, 0), ("gy", 1)), 1)


def margin_depth(rhs):
    return 4 if min(rhs.shape[0], rhs.shape[1]) >= 4 else 2


def deep_border(field, depth):
    return extended(field, ((GZ, 0), ("gy", 1)), depth)


def rhs_border(rhs):
    return extended(rhs, ((GZ, 0), ("gy", 1)), margin_depth(rhs))


def inside_mask(rhs, depth):
    z_cells = rhs.shape[0]
    y_cells = rhs.shape[1]
    z_global = (
        lax.axis_index(GZ) * z_cells - depth + jnp.arange(z_cells + 2 * depth, dtype=jnp.int32)
    )
    y_global = (
        lax.axis_index("gy") * y_cells - depth + jnp.arange(y_cells + 2 * depth, dtype=jnp.int32)
    )
    z_inside = (z_global >= 0) & (z_global < z_cells * lax.axis_size(GZ))
    y_inside = (y_global >= 0) & (y_global < y_cells * lax.axis_size("gy"))
    return (z_inside[:, None, None] & y_inside[None, :, None]).astype(jnp.float32)


def deep_sweeps(rhs, rhs_wide, start):
    depth = margin_depth(rhs)
    inner_rhs = rhs_wide[1:-1, 1:-1, :]
    inside = inside_mask(rhs, depth)
    if start is None:
        padded = jnp.zeros(rhs_wide.shape, jnp.float32)
    else:
        padded = deep_border(start, depth)
    for position in range(len(sweep_order)):
        group, x_order = sweep_order[position]
        if position > 0 and position % depth == 0:
            padded = deep_border(padded[depth:-depth, depth:-depth, :], depth)
        padded = group_update(padded, inner_rhs, 1 - group[0], 1 - group[1], x_order) * inside
    return padded[depth:-depth, depth:-depth, :]


def vcycle_deep(rhs, level):
    if level == LEVELS - 1:
        return deep_sweeps(rhs, rhs_border(rhs), None)
    rhs_wide = rhs_border(rhs)
    first = deep_sweeps(rhs, rhs_wide, None)
    defect = rhs - operate(joint_halo(first))
    coarse = vcycle_deep(defect[::2, ::2, ::2], level + 1)
    start = first.at[::2, ::2, ::2].add(coarse)
    return deep_sweeps(rhs, rhs_wide, start)


def body(right_side):
    precond = vcycle_deep(right_side, 0)
    numer = over_axes(jnp.sum(right_side * precond), GZ_GY)
    image = operate(joint_halo(precond))
    denom = over_axes(jnp.sum(precond * image), GZ_GY)
    alpha = numer / denom
    return (alpha * precond, right_side - alpha * image)


def solution(mesh):
    finer = Mesh(mesh.devices.reshape(12, 4, 2, mesh.shape["gy"]), ("gz_0", "gz_1", "gz_2", "gy"))
    return jax.shard_map(
        body,
        mesh=finer,
        in_specs=(P(GZ, "gy", None),),
        out_specs=(P(GZ, "gy", None), P(GZ, "gy", None)),
        check_vma=False,
    )
```

profile of v0, /device:TPU:66, one launch (start us, length us, event | category | flops | bytes accessed | tf_op | source)
XLA Modules:
  0.0 562.9 jit_solution(1915912460567558003)
XLA Ops:
  14.0 4.6 collective-permute-done.3
  19.3 3.9 scatter_fusion
  32.2 3.9 scatter_fusion.2
  55.1 4.3 collective-permute-done.7
  67.6 3.9 scatter_fusion.5
  80.5 3.9 scatter_fusion.7
  91.5 5.4 collective-permute-start.10
  98.3 4.2 collective-permute-done.11
  116.7 4.0 collective-permute-done.15
  149.2 4.2 collective-permute-done.19
  182.8 4.2 collective-permute-done.23
  201.2 4.0 collective-permute-done.27
  243.4 4.2 collective-permute-done.35
  264.9 4.1 collective-permute-done.39
  273.2 15.2 %scatter_fusion.24 = f32[4,4,128]{2,1,0:T(4,128)S(1)} fusion(f32[4,4,128]{2,1,0:T(4,128)S(1)} %slice.2861, s32[256]{0:T(256)S(1)} %reshape.298, f32[256]{0:T(256)S(1)} %reshape.300), kind=kCustom, calls=%fused_computation.24 | custom fusion | flops 256 | bytes 6144 | tf_op jit(solution)/shard_map/scatter-add | solution.py:138
  335.8 4.1 collective-permute-done.47
  355.9 14.7 %scatter_fusion.41 = f32[16384]{0:T(1024)S(1)} fusion(f32[16384]{0:T(1024)S(1)} %bitcast.39, s32[2048]{0:T(1024)S(1)} %bitcast.40, f32[2048]{0:T(1024)S(1)} %bitcast.41), kind=kCustom, calls=%fused_computation.41 | custom fusion | flops 2048 | bytes 32768
  384.8 4.3 collective-permute-done.51
  391.5 3.9 scatter_fusion.33
  428.3 4.3 collective-permute-done.55
  471.2 4.2 collective-permute-done.59
  476.3 44.0 %all-reduce.240 = (f32[]{:T(128)}, f32[]{:T(128)}) all-reduce(f32[]{:T(128)} %get-tuple-element.3, f32[]{:T(128)} %get-tuple-element.2), channel_id=1, replica_groups=mesh['gz_0'=12,'gz_1'=4,'gz_2'=2,'gy'=8] {'gz_0'}, use_global_device_ids=true, to_apply=%region_43.44 | all-reduce | flops 2 | bytes 16 | tf_op jit(solution)/shard_map/psum | solution.py:39
  520.3 20.5 %all-reduce.242 = (f32[]{:T(128)}, f32[]{:T(128)}) all-reduce(f32[]{:T(128)} %get-tuple-element.4, f32[]{:T(128)} %get-tuple-element.5), channel_id=1, replica_groups=mesh['gz_0'=12,'gz_1'=4,'gz_2'=2,'gy'=8] {'gz_1'}, use_global_device_ids=true, to_apply=%region_44.45 | all-reduce | flops 2 | bytes 16 | tf_op jit(solution)/shard_map/psum | solution.py:39
  543.9 16.0 %all-reduce.241 = (f32[]{:T(128)}, f32[]{:T(128)}) all-reduce(f32[]{:T(128)} %get-tuple-element.10, f32[]{:T(128)} %get-tuple-element.11), channel_id=1, replica_groups=mesh['gz_0'=12,'gz_1'=4,'gz_2'=2,'gy'=8] {'gy'}, use_global_device_ids=true, to_apply=%region_46.47 | all-reduce | flops 2 | bytes 16 | tf_op jit(solution)/shard_map/psum | solution.py:39
  (921 shorter events, 365.2 us)
Async XLA Ops:
  1.4 6.1 %collective-permute-start = (f32[4,8,256]{2,1,0:T(8,128)S(1)}, f32[4,8,256]{2,1,0:T(8,128)S(1)}, u32[]{:S(2)}, u32[]{:S(2)}) collective-permute-start(f32[4,8,256]{2,1,0:T(8,128)S(1)} %get-tuple-element.122), channel_id=1, source_target_pairs={{0,8},{8,16},{16,24},{24,32},{32,40},{40,48},{48,56},{56,64},{64,7... | collective-permute-start | bytes 98312 | tf_op jit(solution)/shard_map/ppermute | solution.py:29
  12.1 6.5 %collective-permute-start.3 = (f32[16,4,256]{2,1,0:T(4,128)S(1)}, f32[16,4,256]{2,1,0:T(4,128)S(1)}, u32[]{:S(2)}, u32[]{:S(2)}) collective-permute-start(f32[16,4,256]{2,1,0:T(4,128)S(1)} %get-tuple-element.104), channel_id=1, source_target_pairs={{1,0},{2,1},{3,2},{4,3},{5,4},{6,5},{7,6},{9,8},{10,9},{11,10},{12... | collective-permute-start | bytes 196616 | tf_op jit(solution)/shard_map/ppermute | solution.py:32
  53.2 6.2 %collective-permute-start.7 = (f32[16,4,256]{2,1,0:T(4,128)S(1)}, f32[16,4,256]{2,1,0:T(4,128)S(1)}, u32[]{:S(2)}, u32[]{:S(2)}) collective-permute-start(f32[16,4,256]{2,1,0:T(4,128)S(1)} %get-tuple-element.102), channel_id=1, source_target_pairs={{1,0},{2,1},{3,2},{4,3},{5,4},{6,5},{7,6},{9,8},{10,9},{11,10},{12... | collective-permute-start | bytes 196616 | tf_op jit(solution)/shard_map/ppermute | solution.py:32
  91.5 6.8 %collective-permute-start.10 = (f32[10,1,256]{2,1,0:T(1,128)S(1)}, f32[10,1,256]{2,1,0:T(1,128)S(1)}, u32[]{:S(2)}, u32[]{:S(2)}) collective-permute-start(f32[10,1,256]{2,1,0:T(1,128)S(1)} %get-tuple-element.113), channel_id=1, source_target_pairs={{0,1},{1,2},{2,3},{3,4},{4,5},{5,6},{6,7},{8,9},{9,10},{10,11},{11... | collective-permute-start | bytes 30728 | tf_op jit(solution)/shard_map/ppermute | solution.py:29
  110.6 6.1 %collective-permute-start.14 = (f32[12,4,128]{2,1,0:T(4,128)S(1)}, f32[12,4,128]{2,1,0:T(4,128)S(1)}, u32[]{:S(2)}, u32[]{:S(2)}) collective-permute-start(f32[12,4,128]{2,1,0:T(4,128)S(1)} %pad_maximum_fusion.20), channel_id=1, source_target_pairs={{0,1},{1,2},{2,3},{3,4},{4,5},{5,6},{6,7},{8,9},{9,10},{10,11},{11... | collective-permute-start | bytes 73736 | tf_op jit(solution)/shard_map/ppermute | solution.py:29
  114.5 6.2 %collective-permute-start.15 = (f32[12,4,128]{2,1,0:T(4,128)S(1)}, f32[12,4,128]{2,1,0:T(4,128)S(1)}, u32[]{:S(2)}, u32[]{:S(2)}) collective-permute-start(f32[12,4,128]{2,1,0:T(4,128)S(1)} %pad_maximum_fusion.20), channel_id=1, source_target_pairs={{1,0},{2,1},{3,2},{4,3},{5,4},{6,5},{7,6},{9,8},{10,9},{11,10},{12... | collective-permute-start | bytes 73736 | tf_op jit(solution)/shard_map/ppermute | solution.py:32
  135.8 6.7 %collective-permute-start.16 = (f32[4,4,128]{2,1,0:T(4,128)S(1)}, f32[4,4,128]{2,1,0:T(4,128)S(1)}, u32[]{:S(2)}, u32[]{:S(2)}) collective-permute-start(f32[4,4,128]{2,1,0:T(4,128)S(1)} %slice_multiply_fusion.2), channel_id=1, source_target_pairs={{0,8},{8,16},{16,24},{24,32},{32,40},{40,48},{48,56},{56,64},{64,7... | collective-permute-start | bytes 24584 | tf_op jit(solution)/shard_map/ppermute | solution.py:29
  147.7 5.7 %collective-permute-start.19 = (f32[12,4,128]{2,1,0:T(4,128)S(1)}, f32[12,4,128]{2,1,0:T(4,128)S(1)}, u32[]{:S(2)}, u32[]{:S(2)}) collective-permute-start(f32[12,4,128]{2,1,0:T(4,128)S(1)} %pad_maximum_fusion.21), channel_id=1, source_target_pairs={{1,0},{2,1},{3,2},{4,3},{5,4},{6,5},{7,6},{9,8},{10,9},{11,10},{12... | collective-permute-start | bytes 73736 | tf_op jit(solution)/shard_map/ppermute | solution.py:32
  169.3 7.1 %collective-permute-start.20 = (f32[1,4,128]{2,1,0:T(4,128)S(1)}, f32[1,4,128]{2,1,0:T(4,128)S(1)}, u32[]{:S(2)}, u32[]{:S(2)}) collective-permute-start(f32[1,4,128]{2,1,0:T(4,128)S(1)} %get-tuple-element.105), channel_id=1, source_target_pairs={{0,8},{8,16},{16,24},{24,32},{32,40},{40,48},{48,56},{56,64},{64,7... | collective-permute-start | bytes 6152 | tf_op jit(solution)/shard_map/ppermute | solution.py:29
  187.5 7.1 %collective-permute-start.24 = (f32[2,2,64]{2,1,0:T(2,128)S(1)}, f32[2,2,64]{2,1,0:T(2,128)S(1)}, u32[]{:S(2)}, u32[]{:S(2)}) collective-permute-start(f32[2,2,64]{2,1,0:T(2,128)S(1)} %slice.2284), channel_id=1, source_target_pairs={{0,8},{8,16},{16,24},{24,32},{32,40},{40,48},{48,56},{56,64},{64,7... | collective-permute-start | bytes 3080 | tf_op jit(solution)/shard_map/ppermute | solution.py:29
  208.5 6.9 %collective-permute-start.28 = (f32[2,2,64]{2,1,0:T(2,128)S(1)}, f32[2,2,64]{2,1,0:T(2,128)S(1)}, u32[]{:S(2)}, u32[]{:S(2)}) collective-permute-start(f32[2,2,64]{2,1,0:T(2,128)S(1)} %slice_multiply_fusion.6), channel_id=1, source_target_pairs={{0,8},{8,16},{16,24},{24,32},{32,40},{40,48},{48,56},{56,64},{64,7... | collective-permute-start | bytes 3080 | tf_op jit(solution)/shard_map/ppermute | solution.py:29
  230.0 6.9 %collective-permute-start.32 = (f32[2,2,64]{2,1,0:T(2,128)S(1)}, f32[2,2,64]{2,1,0:T(2,128)S(1)}, u32[]{:S(2)}, u32[]{:S(2)}) collective-permute-start(f32[2,2,64]{2,1,0:T(2,128)S(1)} %slice_multiply_fusion.5), channel_id=1, source_target_pairs={{0,8},{8,16},{16,24},{24,32},{32,40},{40,48},{48,56},{56,64},{64,7... | collective-permute-start | bytes 3080 | tf_op jit(solution)/shard_map/ppermute | solution.py:29
  251.4 7.0 %collective-permute-start.36 = (f32[2,2,64]{2,1,0:T(2,128)S(1)}, f32[2,2,64]{2,1,0:T(2,128)S(1)}, u32[]{:S(2)}, u32[]{:S(2)}) collective-permute-start(f32[2,2,64]{2,1,0:T(2,128)S(1)} %slice_multiply_fusion.4), channel_id=1, source_target_pairs={{0,8},{8,16},{16,24},{24,32},{32,40},{40,48},{48,56},{56,64},{64,7... | collective-permute-start | bytes 3080 | tf_op jit(solution)/shard_map/ppermute | solution.py:29
  254.7 5.7 %collective-permute-start.37 = (f32[2,2,64]{2,1,0:T(2,128)S(1)}, f32[2,2,64]{2,1,0:T(2,128)S(1)}, u32[]{:S(2)}, u32[]{:S(2)}) collective-permute-start(f32[2,2,64]{2,1,0:T(2,128)S(1)} %slice_multiply_fusion.4), channel_id=1, source_target_pairs={{8,0},{16,8},{24,16},{32,24},{40,32},{48,40},{56,48},{64,56},{72,6... | collective-permute-start | bytes 3080 | tf_op jit(solution)/shard_map/ppermute | solution.py:32
  288.4 6.9 %collective-permute-start.40 = (f32[4,4,128]{2,1,0:T(4,128)S(1)}, f32[4,4,128]{2,1,0:T(4,128)S(1)}, u32[]{:S(2)}, u32[]{:S(2)}) collective-permute-start(f32[4,4,128]{2,1,0:T(4,128)S(1)} %scatter_fusion.24), channel_id=1, source_target_pairs={{0,8},{8,16},{16,24},{24,32},{32,40},{40,48},{48,56},{56,64},{64,7... | collective-permute-start | bytes 24584 | tf_op jit(solution)/shard_map/ppermute | solution.py:29
  291.7 5.7 %collective-permute-start.41 = (f32[4,4,128]{2,1,0:T(4,128)S(1)}, f32[4,4,128]{2,1,0:T(4,128)S(1)}, u32[]{:S(2)}, u32[]{:S(2)}) collective-permute-start(f32[4,4,128]{2,1,0:T(4,128)S(1)} %scatter_fusion.24), channel_id=1, source_target_pairs={{8,0},{16,8},{24,16},{32,24},{40,32},{48,40},{56,48},{64,56},{72,6... | collective-permute-start | bytes 24584 | tf_op jit(solution)/shard_map/ppermute | solution.py:32
  300.5 5.7 %collective-permute-start.43 = (f32[12,4,128]{2,1,0:T(4,128)S(1)}, f32[12,4,128]{2,1,0:T(4,128)S(1)}, u32[]{:S(2)}, u32[]{:S(2)}) collective-permute-start(f32[12,4,128]{2,1,0:T(4,128)S(1)} %constant_dynamic-update-slice_fusion.3), channel_id=1, source_target_pairs={{1,0},{2,1},{3,2},{4,3},{5,4},{6,5},{7,6},{9,8},{10,9},{11,10},{12... | collective-permute-start | bytes 73736 | tf_op jit(solution)/shard_map/ppermute | solution.py:32
  322.1 7.0 %collective-permute-start.44 = (f32[4,4,128]{2,1,0:T(4,128)S(1)}, f32[4,4,128]{2,1,0:T(4,128)S(1)}, u32[]{:S(2)}, u32[]{:S(2)}) collective-permute-start(f32[4,4,128]{2,1,0:T(4,128)S(1)} %slice_multiply_fusion.1), channel_id=1, source_target_pairs={{0,8},{8,16},{16,24},{24,32},{32,40},{40,48},{48,56},{56,64},{64,7... | collective-permute-start | bytes 24584 | tf_op jit(solution)/shard_map/ppermute | solution.py:29
  334.2 5.7 %collective-permute-start.47 = (f32[12,4,128]{2,1,0:T(4,128)S(1)}, f32[12,4,128]{2,1,0:T(4,128)S(1)}, u32[]{:S(2)}, u32[]{:S(2)}) collective-permute-start(f32[12,4,128]{2,1,0:T(4,128)S(1)} %pad_maximum_fusion.26), channel_id=1, source_target_pairs={{1,0},{2,1},{3,2},{4,3},{5,4},{6,5},{7,6},{9,8},{10,9},{11,10},{12... | collective-permute-start | bytes 73736 | tf_op jit(solution)/shard_map/ppermute | solution.py:32
  370.7 7.0 %collective-permute-start.48 = (f32[4,8,256]{2,1,0:T(8,128)S(1)}, f32[4,8,256]{2,1,0:T(8,128)S(1)}, u32[]{:S(2)}, u32[]{:S(2)}) collective-permute-start(f32[4,8,256]{2,1,0:T(8,128)S(1)} %reshape.152), channel_id=1, source_target_pairs={{0,8},{8,16},{16,24},{24,32},{32,40},{40,48},{48,56},{56,64},{64,7... | collective-permute-start | bytes 98312 | tf_op jit(solution)/shard_map/ppermute | solution.py:29
  382.9 6.2 %collective-permute-start.51 = (f32[16,4,256]{2,1,0:T(4,128)S(1)}, f32[16,4,256]{2,1,0:T(4,128)S(1)}, u32[]{:S(2)}, u32[]{:S(2)}) collective-permute-start(f32[16,4,256]{2,1,0:T(4,128)S(1)} %get-tuple-element.100), channel_id=1, source_target_pairs={{1,0},{2,1},{3,2},{4,3},{5,4},{6,5},{7,6},{9,8},{10,9},{11,10},{12... | collective-permute-start | bytes 196616 | tf_op jit(solution)/shard_map/ppermute | solution.py:32
  414.2 7.0 %collective-permute-start.52 = (f32[4,8,256]{2,1,0:T(8,128)S(1)}, f32[4,8,256]{2,1,0:T(8,128)S(1)}, u32[]{:S(2)}, u32[]{:S(2)}) collective-permute-start(f32[4,8,256]{2,1,0:T(8,128)S(1)} %get-tuple-element.89), channel_id=1, source_target_pairs={{0,8},{8,16},{16,24},{24,32},{32,40},{40,48},{48,56},{56,64},{64,7... | collective-permute-start | bytes 98312 | tf_op jit(solution)/shard_map/ppermute | solution.py:29
  426.4 6.2 %collective-permute-start.55 = (f32[16,4,256]{2,1,0:T(4,128)S(1)}, f32[16,4,256]{2,1,0:T(4,128)S(1)}, u32[]{:S(2)}, u32[]{:S(2)}) collective-permute-start(f32[16,4,256]{2,1,0:T(4,128)S(1)} %get-tuple-element.98), channel_id=1, source_target_pairs={{1,0},{2,1},{3,2},{4,3},{5,4},{6,5},{7,6},{9,8},{10,9},{11,10},{12... | collective-permute-start | bytes 196616 | tf_op jit(solution)/shard_map/ppermute | solution.py:32
  457.7 7.2 %collective-permute-start.56 = (f32[1,8,256]{2,1,0:T(8,128)S(1)}, f32[1,8,256]{2,1,0:T(8,128)S(1)}, u32[]{:S(2)}, u32[]{:S(2)}) collective-permute-start(f32[1,8,256]{2,1,0:T(8,128)S(1)} %get-tuple-element.87), channel_id=1, source_target_pairs={{0,8},{8,16},{16,24},{24,32},{32,40},{40,48},{48,56},{56,64},{64,7... | collective-permute-start | bytes 24584 | tf_op jit(solution)/shard_map/ppermute | solution.py:29
  (39 other events, 195.6 us)
where the time goes:
time: 573 us; the launch traced here: 563 us
  starting transfers between devices  170 us (30%)
  local copies, waits for them, and re-layouts  166 us (29%)
  waiting for transfers between devices  91.1 us (16%)
  blocking collectives  83.6 us (15%)
  other arithmetic  45.2 us (8%)
  between operations  7.53 us (1%)
    scatter x40, local copies, waits for them, and re-layouts, group_update(): padded.at[1 + z_par:z_cells + z_par:2, 1 + y_par:y_cells + y_par:2, :]  103 us
    ppermute x30, starting transfers between devices, extended(): lax.ppermute(lax.slice_in_dim(block, block.shape[dim] - width, None, axis...  97.6 us
    ppermute x30, waiting for transfers between devices, extended(): lax.ppermute(lax.slice_in_dim(block, 0, width, axis=dim), axis, backward)  88.7 us
    psum x4, blocking collectives, over_axes(): value = lax.psum(value, axis)  83.6 us
    ppermute x30, starting transfers between devices, extended(): lax.ppermute(lax.slice_in_dim(block, 0, width, axis=dim), axis, backward)  72 us
    slice x296, local copies, waits for them, and re-layouts, group_update(): padded[1 + z_par + z_step:z_cells + z_par + z_step:2, 1 + y_par + y_step:...  42.2 us
    scatter-add x1, other arithmetic, vcycle_deep(): start = first.at[::2, ::2, ::2].add(coarse)  15.2 us
    unnamed x4, other arithmetic  14.9 us
  transfers between devices with their start and end apart: 60, of which 36 were waited for; matrix products, arithmetic and copies ran while one was open for 0% of the time, Pallas kernels for 0%

commit v1 on v0

v1 whole, which is shorter than its diff:
```python
import functools

import jax
import jax.numpy as jnp
from jax import lax
from jax.experimental import pallas as pl
from jax.experimental.pallas import tpu as pltpu
from jax.sharding import PartitionSpec as P

MESH = pl.DeviceIdType.MESH
F32 = jnp.float32
INV = 1.0 / 26.0
NX_CHIPS = 4
CORES = 2

SWEEP = [
    ((0, 0), (0, 1)),
    ((0, 1), (0, 1)),
    ((1, 0), (0, 1)),
    ((1, 1), (0, 1, 0)),
    ((1, 0), (1, 0)),
    ((0, 1), (1, 0)),
    ((0, 0), (1, 0)),
]
PRE_ROWS = [(1, 11), (1, 10), (2, 10), (2, 9), (3, 9), (3, 8), (4, 8)]
POST_ROWS = [(1, 12), (1, 11), (2, 11), (2, 10), (3, 10), (3, 9), (4, 9)]


def lanes(shape):
    return lax.broadcasted_iota(jnp.int32, shape, len(shape) - 1)


def sublanes(shape):
    return lax.broadcasted_iota(jnp.int32, shape, len(shape) - 2)


def from_left(u, step=1):
    return jnp.where(lanes(u.shape) >= step, pltpu.roll(u, step, u.ndim - 1), 0.0)


def from_right(u, step=1):
    return jnp.where(lanes(u.shape) < 128 - step, pltpu.roll(u, 128 - step, u.ndim - 1), 0.0)


def both_sides(u, step=1):
    return from_left(u, step) + from_right(u, step)


def down(u):
    return pltpu.roll(u, 1, u.ndim - 2)


def up(u):
    return pltpu.roll(u, 7, u.ndim - 2)


def remote(src, dst, send, recv, where):
    copy = pltpu.make_async_remote_copy(
        src_ref=src, dst_ref=dst, send_sem=send, recv_sem=recv, device_id=where, device_id_type=MESH
    )
    return copy


def kernel(
    ngz, ngy, r_ref, sol_ref, res_ref,
    rw, rd, f0, v0, p0, mk, own, fw, dcb, dall, f1, v1, p1, f2, v2, vc, stage, prec, imag, sb, ar1, ar2,
    rs, rr, fs, fr, cs, cr, s1, r1, s2, r2,
):
    gz = lax.axis_index("gz")
    gy = lax.axis_index("gy")
    nz = ngz // (NX_CHIPS * CORES)
    core = lax.rem(gz, CORES)
    chip_x = lax.rem(gz // CORES, NX_CHIPS)
    chip_z = gz // (CORES * NX_CHIPS)

    def at(dz, dy):
        return (lax.rem(gz + dz + ngz, ngz), lax.rem(gy + dy + ngy, ngy))

    def along_z(dc, dz):
        z = lax.rem(chip_z + dz + nz, nz)
        return ((z * NX_CHIPS + chip_x) * CORES + lax.rem(core + dc, CORES), gy)

    def along_xy(dx, dy):
        x = lax.rem(chip_x + dx + NX_CHIPS, NX_CHIPS)
        return ((chip_z * NX_CHIPS + x) * CORES + core, lax.rem(gy + dy + ngy, ngy))

    coarse_sends = [
        (slot, dz, dy)
        for dy in range(ngy)
        for slot, dz in ((2, 0), (1, 1), (3, -1), (0, 2))
        if not (dz == 0 and dy == 0)
    ]
    first_group = [(c, z) for z in range(nz) for c in range(CORES) if (c, z) != (0, 0)]
    second_group = [(x, y) for y in range(ngy) for x in range(NX_CHIPS) if (x, y) != (0, 0)]
    halo = [(dz, dy) for dz in (0, 1, -1) for dy in (0, 1, -1) if (dz, dy) != (0, 0)]

    barrier = pltpu.get_barrier_semaphore()
    for slot, dz, dy in coarse_sends:
        pl.semaphore_signal(barrier, inc=1, device_id=at(-dz, -dy), device_id_type=MESH)
    for c, z in first_group:
        pl.semaphore_signal(barrier, inc=1, device_id=along_z(-c + CORES, -z), device_id_type=MESH)
    for x, y in second_group:
        pl.semaphore_signal(barrier, inc=1, device_id=along_xy(-x, -y), device_id_type=MESH)

    for yb in range(3):
        for zi in (0, 14, 15):
            rw[yb, zi] = jnp.zeros((8, 256), F32)
        fw[yb, :, 120:128, :] = jnp.zeros((2, 8, 128), F32)
    fw[1, :, 24:88, :] = jnp.zeros((2, 64, 128), F32)
    rw[1, 3:11] = r_ref[...]
    dall[:, 0:8, :] = jnp.zeros((ngy, 8, 128), F32)
    v0[...] = jnp.zeros(v0.shape, F32)
    p0[...] = jnp.zeros(p0.shape, F32)
    v1[...] = jnp.zeros(v1.shape, F32)
    p1[...] = jnp.zeros(p1.shape, F32)
    v2[...] = jnp.zeros(v2.shape, F32)

    sub = sublanes((8, 128))
    for zp in range(2):
        z = gz * 8 + 2 * sub - (2 + zp)
        z_in = ((z >= 0) & (z < ngz * 8)).astype(F32)
        low = jnp.where(gy > 0, 1.0, 0.0).astype(F32)
        high = jnp.where(gy < ngy - 1, 1.0, 0.0).astype(F32)
        mk[zp, 0:4] = jnp.broadcast_to(z_in * low, (4, 8, 128))
        mk[zp, 4:8] = jnp.broadcast_to(z_in, (4, 8, 128))
        mk[zp, 8:12] = jnp.broadcast_to(z_in * high, (4, 8, 128))

    def own_rows(zp, shape):
        s = sublanes(shape)
        return (s >= 1 + zp) & (s < 5 + zp)

    pl.semaphore_wait(barrier, len(coarse_sends) + len(first_group) + len(second_group))

    rhs_rows = {0: (0, 8, 3), 1: (6, 2, 1), -1: (0, 3, 11)}
    rhs_copies = []
    for k, (dz, dy) in enumerate(halo):
        z_from, count, z_to = rhs_rows[dz]
        copy = remote(
            r_ref.at[pl.ds(z_from, count)], rw.at[1 - dy, pl.ds(z_to, count)], rs.at[k], rr.at[k], at(dz, dy)
        )
        copy.start()
        rhs_copies.append(copy)

    row = lax.broadcasted_iota(jnp.int32, (256, 256), 0)
    col = lax.broadcasted_iota(jnp.int32, (256, 256), 1)
    split = (row == jnp.where(col < 128, 2 * col, 2 * col - 255)).astype(F32)
    merge = (col == jnp.where(row < 128, 2 * row, 2 * row - 255)).astype(F32)

    def permuted(block, matrix):
        return lax.dot_general(
            block, matrix, (((1,), (0,)), ((), ())), precision=lax.Precision.HIGHEST, preferred_element_type=F32
        )

    for copy in rhs_copies:
        copy.wait_recv()
    for yb in range(3):
        both = permuted(rw[yb].reshape(128, 256), split)
        rd[yb, 0] = both[:, :128]
        rd[yb, 1] = both[:, 128:]

    def window(zp, yp, i):
        return i // 4, pl.ds(8 * (1 - zp) + 2 * (i % 4) + yp, 8, stride=16)

    for zp in range(2):
        for yp in range(2):
            for xp in range(2):
                for i in range(12):
                    yb, rows = window(zp, yp, i)
                    f0[zp, yp, xp, i] = rd[yb, xp, rows, :]

    def pair0(zp, c):
        return c + (down(c) if zp == 0 else up(c))

    def outer0(zp, yp, lo, hi):
        a = -1 if yp == 0 else 0
        sums = []
        for xp in range(2):
            s = v0[zp, 1 - yp, xp, lo + a : hi + a] + v0[zp, 1 - yp, xp, lo + a + 1 : hi + a + 1]
            q = p0[1 - zp, 1 - yp, xp, lo + a : hi + a] + p0[1 - zp, 1 - yp, xp, lo + a + 1 : hi + a + 1]
            sums.append(s + q + p0[1 - zp, yp, xp, lo:hi])
        return sums

    def around0(s, c, xp):
        other = s[1 - xp] + c[1 - xp]
        return s[xp] + (other + (from_left(other) if xp == 0 else from_right(other)))

    def phase0(group, order, lo, hi):
        zp, yp = group
        s = outer0(zp, yp, lo, hi)
        c = [v0[zp, yp, 0, lo:hi], v0[zp, yp, 1, lo:hi]]
        scale = mk[zp, lo:hi] * INV
        for xp in order:
            c[xp] = (around0(s, c, xp) + f0[zp, yp, xp, lo:hi]) * scale
        for xp in range(2):
            v0[zp, yp, xp, lo:hi] = c[xp]
            p0[zp, yp, xp, lo:hi] = pair0(zp, c[xp])

    for (group, order), (lo, hi) in zip(SWEEP, PRE_ROWS):
        phase0(group, order, lo, hi)

    for zp in range(2):
        for yp in range(2):
            for xp in range(2):
                for i in range(4, 8):
                    own[xp, window(zp, yp, i)[1], :] = v0[zp, yp, xp, i]
    field_rows = {0: (3, 8, 3), 1: (8, 3, 0), -1: (3, 4, 11)}
    field_copies = []
    s = outer0(0, 0, 4, 8)
    c = [v0[0, 0, 0, 4:8], v0[0, 0, 1, 4:8]]
    defect = up(f0[0, 0, 0, 4:8] - (26.0 * c[0] - around0(s, c, 0)))
    for i in range(4):
        dcb[pl.ds(i, 8, stride=4), :] = defect[i]
    for k, (dz, dy) in enumerate(halo):
        z_from, count, z_to = field_rows[dz]
        copy = remote(
            own.at[:, pl.ds(8 * z_from, 8 * count), :],
            fw.at[1 - dy, :, pl.ds(8 * z_to, 8 * count), :],
            fs.at[k], fr.at[k], at(dz, dy),
        )
        copy.start()
        field_copies.append(copy)
    coarse_copies = []
    for k, (slot, dz, dy) in enumerate(coarse_sends):
        first, count = (8, 8) if slot == 0 else (0, 16)
        copy = remote(
            dcb.at[pl.ds(first, count), :], dall.at[gy, pl.ds(16 * slot + first, count), :],
            cs.at[k], cr.at[k], at(dz, dy),
        )
        copy.start()
        coarse_copies.append(copy)
    dall[gy, 32:48, :] = dcb[0:16, :]

    for copy in field_copies:
        copy.wait_recv()
    for zp in range(2):
        for yp in range(2):
            for xp in range(2):
                for i in range(12):
                    yb, rows = window(zp, yp, i)
                    value = fw[yb, xp, rows, :] * mk[zp, i]
                    if yb == 1:
                        value = jnp.where(own_rows(zp, (8, 128)), v0[zp, yp, xp, i], value)
                    v0[zp, yp, xp, i] = value
                    if zp == 1:
                        p0[zp, yp, xp, i] = pair0(zp, value)

    for copy in coarse_copies:
        copy.wait_recv()

    n1 = 2 * ngy
    for zp in range(2):
        for yp in range(2):
            for i in range(n1):
                f1[zp, yp, i] = dall[i // 2, pl.ds(2 * (i % 2) + yp + 4 * zp, 8, stride=8), :]

    scale1 = []
    for zp in range(2):
        z = gz * 4 + 2 * sub - (8 - zp)
        scale1.append(jnp.where((z >= 0) & (z < ngz * 4), INV, 0.0).astype(F32)[None])

    def pair1(zp, c):
        return c + (up(c) if zp == 0 else down(c))

    def outer1(zp, yp):
        a = 0 if yp == 0 else 1
        s = v1[zp, 1 - yp, a : a + n1] + v1[zp, 1 - yp, a + 1 : a + 1 + n1]
        q = p1[1 - zp, 1 - yp, a : a + n1] + p1[1 - zp, 1 - yp, a + 1 : a + 1 + n1]
        return s + q + p1[1 - zp, yp, 1 : 1 + n1]

    def phase1(group, order):
        zp, yp = group
        s = outer1(zp, yp)
        c = v1[zp, yp, 1 : 1 + n1]
        base = s + f1[zp, yp]
        parity = lax.rem(lanes(c.shape), 2)
        for xp in order:
            c = jnp.where(parity == xp, (base + both_sides(s + c)) * scale1[zp], c)
        v1[zp, yp, 1 : 1 + n1] = c
        p1[zp, yp, 1 : 1 + n1] = pair1(zp, c)

    for group, order in SWEEP:
        phase1(group, order)

    n2 = ngy
    s = outer1(0, 0)
    c = v1[0, 0, 1 : 1 + n1]
    even = lax.rem(lanes(c.shape), 2) == 0
    defect = jnp.where(even, f1[0, 0] - (26.0 * c - (s + both_sides(s + c))), 0.0)
    for i in range(n1):
        f2[i % 2, i // 2] = defect[i]
    z = gz * 2 + sub - 4
    scale2 = jnp.where((z >= 0) & (z < ngz * 2), INV, 0.0).astype(F32)[None]

    for group, order in SWEEP:
        zp, yp = group
        a = 0 if yp == 0 else 1
        c = v2[yp, 1 : 1 + n2]
        side = v2[1 - yp, a : a + n2] + v2[1 - yp, a + 1 : a + 1 + n2]
        column = side + c
        s = side + (down(column) + up(column))
        base = s + f2[yp]
        layer = lax.rem(sublanes(c.shape), 2) == zp
        place = lax.rem(lanes(c.shape), 4)
        for xp in order:
            c = jnp.where(layer & (place == 2 * xp), (base + both_sides(s + c, 2)) * scale2, c)
        v2[yp, 1 : 1 + n2] = c

    held = sublanes((8, 128))
    mine = (held >= 4) & (held < 6)
    for i in range(n1):
        value = v1[0, 0, 1 + i] + jnp.where(mine, v2[i % 2, 1 + i // 2], 0.0)
        v1[0, 0, 1 + i] = value
        p1[0, 0, 1 + i] = pair1(0, value)
    for group, order in SWEEP:
        phase1(group, order)

    for i in range(4):
        for zp in range(2):
            vc[i, pl.ds(zp, 8, stride=2), :] = v1[zp, i % 2, 1 + 2 * gy + i // 2]
    for i in range(4):
        v0[0, 0, 0, 4 + i] += jnp.where(own_rows(0, (8, 128)), vc[i, 7:15, :], 0.0)

    for (group, order), (lo, hi) in zip(SWEEP, POST_ROWS):
        phase0(group, order, lo, hi)

    numer = jnp.zeros((8, 128), F32)
    denom = jnp.zeros((8, 128), F32)
    images = {}
    for zp in range(2):
        for yp in range(2):
            s = outer0(zp, yp, 4, 8)
            c = [v0[zp, yp, 0, 4:8], v0[zp, yp, 1, 4:8]]
            mine = own_rows(zp, (8, 128))
            top, bottom = 0.0, 0.0
            for xp in range(2):
                image = 26.0 * c[xp] - around0(s, c, xp)
                images[zp, yp, xp] = image
                top = top + jnp.sum(c[xp] * f0[zp, yp, xp, 4:8], axis=0)
                bottom = bottom + jnp.sum(c[xp] * image, axis=0)
            numer = numer + jnp.where(mine, top, 0.0)
            denom = denom + jnp.where(mine, bottom, 0.0)
    lower = lanes((8, 128)) < 64
    both = jnp.where(lower, numer + pltpu.roll(numer, 64, 1), denom + pltpu.roll(denom, 64, 1))
    part = jnp.sum(both, axis=0, keepdims=True)
    sb[0] = part
    first_copies = []
    for k, (c, z) in enumerate(first_group):
        copy = remote(sb.at[0], ar1.at[k], s1.at[k], r1.at[k], along_z(c, z))
        copy.start()
        first_copies.append(copy)

    for zp in range(2):
        for yp in range(2):
            for xp in range(2):
                for i in range(4):
                    rows = window(zp, yp, 4 + i)[1]
                    stage[0, xp, rows, :] = v0[zp, yp, xp, 4 + i]
                    stage[1, xp, rows, :] = images[zp, yp, xp][i]
    for t, target in enumerate((prec, imag)):
        block = jnp.concatenate([stage[t, 0, 24:88, :], stage[t, 1, 24:88, :]], axis=1)
        target[...] = permuted(block, merge).reshape(8, 8, 256)

    for copy in first_copies:
        copy.wait_recv()
    part = part + jnp.sum(ar1[...], axis=0)
    sb[1] = part
    second_copies = []
    for k, (x, y) in enumerate(second_group):
        copy = remote(sb.at[1], ar2.at[k], s2.at[k], r2.at[k], along_xy(x, y))
        copy.start()
        second_copies.append(copy)
    for copy in second_copies:
        copy.wait_recv()
    part = part + jnp.sum(ar2[...], axis=0)
    left = lanes((1, 128)) < 64
    total_n = jnp.sum(jnp.where(left, part, 0.0), axis=1, keepdims=True)
    total_d = jnp.sum(jnp.where(left, 0.0, part), axis=1, keepdims=True)
    alpha = (total_n / total_d)[:, :, None]
    sol_ref[...] = alpha * prec[...]
    res_ref[...] = r_ref[...] - alpha * imag[...]

    for copy in rhs_copies + field_copies + coarse_copies + first_copies + second_copies:
        copy.wait_send()


def solution(mesh):
    ngz, ngy = mesh.shape["gz"], mesh.shape["gy"]
    nz = ngz // (NX_CHIPS * CORES)
    coarse = 4 * ngy - 1
    one = nz * CORES - 1
    two = NX_CHIPS * ngy - 1

    def body(right_side):
        out = jax.ShapeDtypeStruct(right_side.shape, F32)
        vm = pltpu.VMEM
        dma = pltpu.SemaphoreType.DMA
        return pl.pallas_call(
            functools.partial(kernel, ngz, ngy),
            name="cg_iteration",
            out_shape=(out, out),
            in_specs=[pl.BlockSpec(memory_space=pltpu.VMEM)],
            out_specs=(pl.BlockSpec(memory_space=pltpu.VMEM), pl.BlockSpec(memory_space=pltpu.VMEM)),
            scratch_shapes=[
                vm((3, 16, 8, 256), F32),
                vm((3, 2, 128, 128), F32),
                vm((2, 2, 2, 12, 8, 128), F32),
                vm((2, 2, 2, 12, 8, 128), F32),
                vm((2, 2, 2, 12, 8, 128), F32),
                vm((2, 12, 8, 128), F32),
                vm((2, 128, 128), F32),
                vm((3, 2, 128, 128), F32),
                vm((32, 128), F32),
                vm((ngy, 64, 128), F32),
                vm((2, 2, 2 * ngy, 8, 128), F32),
                vm((2, 2, 2 * ngy + 2, 8, 128), F32),
                vm((2, 2, 2 * ngy + 2, 8, 128), F32),
                vm((2, ngy, 8, 128), F32),
                vm((2, ngy + 2, 8, 128), F32),
                vm((4, 16, 128), F32),
                vm((2, 2, 128, 128), F32),
                vm((8, 8, 256), F32),
                vm((8, 8, 256), F32),
                vm((2, 1, 128), F32),
                vm((one, 1, 128), F32),
                vm((two, 1, 128), F32),
                dma((8,)), dma((8,)), dma((8,)), dma((8,)), dma((coarse,)), dma((coarse,)),
                dma((one,)), dma((one,)), dma((two,)), dma((two,)),
            ],
            compiler_params=pltpu.CompilerParams(collective_id=0, has_side_effects=True),
        )(right_side)

    return jax.shard_map(
        body,
        mesh=mesh,
        in_specs=(P("gz", "gy", None),),
        out_specs=(P("gz", "gy", None), P("gz", "gy", None)),
        check_vma=False,
    )
```

time: 573 us -> 59 us (0.10)
  the two profiles are of different devices: /device:TPU:66 before, /device:TPU:1 now
where the time goes in v1:
time: 59 us; the launch traced here: 58.8 us
  Pallas kernels  56 us (95%)
  local copies, waits for them, and re-layouts  2.14 us (4%)
  between operations  0.65 us (1%)
    pallas_call x1, Pallas kernels, body(): pl.pallas_call(functools.partial(kernel, ngz, ngy), name='cg_iteration',...  56 us
    unnamed x4, local copies, waits for them, and re-layouts  2.14 us

profile of v1, /device:TPU:1, one launch (start us, length us, event | category | flops | bytes accessed | tf_op | source)
XLA Modules:
  0.0 58.8 jit_solution(17933255603377411828)
XLA Ops:
  0.6 56.0 %cg_iteration.1 = (f32[8,8,256]{2,1,0:T(8,128)}, f32[8,8,256]{2,1,0:T(8,128)}) custom-call(f32[8,8,256]{2,1,0:T(8,128)} %r_ref.1), custom_call_target="tpu_custom_call" | custom-call | tf_op jit(solution)/shard_map/cg_iteration/pallas_call | solution.py:397
  56.6 0.0 copy-start
  56.6 1.5 %copy.5 = f32[8,8,256]{2,1,0:T(8,128)} copy(f32[8,8,256]{2,1,0:T(8,128)} %get-tuple-element.4) | data formatting | bytes 131072
  58.1 0.0 copy-done
  58.1 0.6 %copy.6 = f32[8,8,256]{2,1,0:T(8,128)} copy(f32[8,8,256]{2,1,0:T(8,128)S(1)} %copy-done) | data formatting | bytes 131072
Async XLA Ops:
  56.6 1.5 %copy-start = (f32[8,8,256]{2,1,0:T(8,128)S(1)}, f32[8,8,256]{2,1,0:T(8,128)}, u32[]{:S(2)}) copy-start(f32[8,8,256]{2,1,0:T(8,128)} %get-tuple-element.5) | copy-start | bytes 196612

commit v2 on v1

--- a/solution.py
+++ b/solution.py
@@ -62,9 +62,9 @@
 
 
 def kernel(
-    ngz, ngy, r_ref, sol_ref, res_ref,
-    rw, rd, f0, v0, p0, mk, own, fw, dcb, dall, f1, v1, p1, f2, v2, vc, stage, prec, imag, sb, ar1, ar2,
-    rs, rr, fs, fr, cs, cr, s1, r1, s2, r2,
+    ngz, ngy, r_hbm, prec_hbm, imag_hbm, alpha_ref,
+    rin, ownr, rd, f0, v0, p0, mk, own, fw, dcb, dall, f1, v1, p1, f2, v2, vc, stage, prec, imag, sb, ar1, ar2,
+    io, rs, rr, fs, fr, cs, cr, s1, r1, s2, r2,
 ):
     gz = lax.axis_index("gz")
     gy = lax.axis_index("gy")
@@ -74,40 +74,61 @@
     chip_z = gz // (CORES * NX_CHIPS)
 
     def at(dz, dy):
-        return (lax.rem(gz + dz + ngz, ngz), lax.rem(gy + dy + ngy, ngy))
+        return (lax.rem(gz + dz % ngz, ngz), lax.rem(gy + dy % ngy, ngy))
 
     def along_z(dc, dz):
-        z = lax.rem(chip_z + dz + nz, nz)
-        return ((z * NX_CHIPS + chip_x) * CORES + lax.rem(core + dc, CORES), gy)
+        z = lax.rem(chip_z + dz % nz, nz)
+        return ((z * NX_CHIPS + chip_x) * CORES + lax.rem(core + dc % CORES, CORES), gy)
 
     def along_xy(dx, dy):
-        x = lax.rem(chip_x + dx + NX_CHIPS, NX_CHIPS)
-        return ((chip_z * NX_CHIPS + x) * CORES + core, lax.rem(gy + dy + ngy, ngy))
+        x = lax.rem(chip_x + dx % NX_CHIPS, NX_CHIPS)
+        return ((chip_z * NX_CHIPS + x) * CORES + core, lax.rem(gy + dy % ngy, ngy))
 
     coarse_sends = [
         (slot, dz, dy)
-        for dy in range(ngy)
+        for dy in sorted(range(ngy), key=lambda d: -min(d, ngy - d))
         for slot, dz in ((2, 0), (1, 1), (3, -1), (0, 2))
         if not (dz == 0 and dy == 0)
     ]
     first_group = [(c, z) for z in range(nz) for c in range(CORES) if (c, z) != (0, 0)]
+    first_group.sort(key=lambda g: -min(g[1], nz - g[1]))
     second_group = [(x, y) for y in range(ngy) for x in range(NX_CHIPS) if (x, y) != (0, 0)]
+    second_group.sort(key=lambda g: -min(g[1], ngy - g[1]) - min(g[0], NX_CHIPS - g[0]))
     halo = [(dz, dy) for dz in (0, 1, -1) for dy in (0, 1, -1) if (dz, dy) != (0, 0)]
 
+    load = pltpu.make_async_copy(r_hbm, rin, io.at[0])
+    load.start()
+
     barrier = pltpu.get_barrier_semaphore()
+    for c, z in first_group:
+        pl.semaphore_signal(barrier, inc=1, device_id=along_z(-c, -z), device_id_type=MESH)
+    for x, y in second_group:
+        pl.semaphore_signal(barrier, inc=1, device_id=along_xy(-x, -y), device_id_type=MESH)
     for slot, dz, dy in coarse_sends:
         pl.semaphore_signal(barrier, inc=1, device_id=at(-dz, -dy), device_id_type=MESH)
-    for c, z in first_group:
-        pl.semaphore_signal(barrier, inc=1, device_id=along_z(-c + CORES, -z), device_id_type=MESH)
-    for x, y in second_group:
-        pl.semaphore_signal(barrier, inc=1, device_id=along_xy(-x, -y), device_id_type=MESH)
+
+    row = lax.broadcasted_iota(jnp.int32, (256, 256), 0)
+    col = lax.broadcasted_iota(jnp.int32, (256, 256), 1)
+    split = (row == jnp.where(col < 128, 2 * col, 2 * col - 255)).astype(F32)
+    merge = (col == jnp.where(row < 128, 2 * row, 2 * row - 255)).astype(F32)
+
+    def permuted(block, matrix):
+        return lax.dot_general(
+            block, matrix, (((1,), (0,)), ((), ())), precision=lax.Precision.HIGHEST, preferred_element_type=F32
+        )
+
+    load.wait()
+    both = permuted(rin[...].reshape(64, 256), split)
+    for xp in range(2):
+        part = both[:, 128 * xp : 128 * xp + 128]
+        ownr[xp] = part
+        rd[1, xp, 24:88, :] = part
 
     for yb in range(3):
-        for zi in (0, 14, 15):
-            rw[yb, zi] = jnp.zeros((8, 256), F32)
+        rd[yb, :, 0:8, :] = jnp.zeros((2, 8, 128), F32)
+        rd[yb, :, 112:128, :] = jnp.zeros((2, 16, 128), F32)
         fw[yb, :, 120:128, :] = jnp.zeros((2, 8, 128), F32)
     fw[1, :, 24:88, :] = jnp.zeros((2, 64, 128), F32)
-    rw[1, 3:11] = r_ref[...]
     dall[:, 0:8, :] = jnp.zeros((ngy, 8, 128), F32)
     v0[...] = jnp.zeros(v0.shape, F32)
     p0[...] = jnp.zeros(p0.shape, F32)
@@ -131,32 +152,22 @@
 
     pl.semaphore_wait(barrier, len(coarse_sends) + len(first_group) + len(second_group))
 
-    rhs_rows = {0: (0, 8, 3), 1: (6, 2, 1), -1: (0, 3, 11)}
-    rhs_copies = []
-    for k, (dz, dy) in enumerate(halo):
-        z_from, count, z_to = rhs_rows[dz]
-        copy = remote(
-            r_ref.at[pl.ds(z_from, count)], rw.at[1 - dy, pl.ds(z_to, count)], rs.at[k], rr.at[k], at(dz, dy)
-        )
-        copy.start()
-        rhs_copies.append(copy)
-
-    row = lax.broadcasted_iota(jnp.int32, (256, 256), 0)
-    col = lax.broadcasted_iota(jnp.int32, (256, 256), 1)
-    split = (row == jnp.where(col < 128, 2 * col, 2 * col - 255)).astype(F32)
-    merge = (col == jnp.where(row < 128, 2 * row, 2 * row - 255)).astype(F32)
-
-    def permuted(block, matrix):
-        return lax.dot_general(
-            block, matrix, (((1,), (0,)), ((), ())), precision=lax.Precision.HIGHEST, preferred_element_type=F32
-        )
-
+    def border(source, target, rows, sends, arrivals):
+        copies = []
+        for k, (dz, dy) in enumerate(halo):
+            z_from, count, z_to = rows[dz]
+            copy = remote(
+                source.at[:, pl.ds(8 * z_from, 8 * count), :],
+                target.at[1 - dy, :, pl.ds(8 * z_to, 8 * count), :],
+                sends.at[k], arrivals.at[k], at(dz, dy),
+            )
+            copy.start()
+            copies.append(copy)
+        return copies
+
+    rhs_copies = border(ownr, rd, {0: (0, 8, 3), 1: (6, 2, 1), -1: (0, 3, 11)}, rs, rr)
     for copy in rhs_copies:
         copy.wait_recv()
-    for yb in range(3):
-        both = permuted(rw[yb].reshape(128, 256), split)
-        rd[yb, 0] = both[:, :128]
-        rd[yb, 1] = both[:, 128:]
 
     def window(zp, yp, i):
         return i // 4, pl.ds(8 * (1 - zp) + 2 * (i % 4) + yp, 8, stride=16)
@@ -198,27 +209,16 @@
     for (group, order), (lo, hi) in zip(SWEEP, PRE_ROWS):
         phase0(group, order, lo, hi)
 
-    for zp in range(2):
-        for yp in range(2):
-            for xp in range(2):
-                for i in range(4, 8):
-                    own[xp, window(zp, yp, i)[1], :] = v0[zp, yp, xp, i]
-    field_rows = {0: (3, 8, 3), 1: (8, 3, 0), -1: (3, 4, 11)}
-    field_copies = []
     s = outer0(0, 0, 4, 8)
     c = [v0[0, 0, 0, 4:8], v0[0, 0, 1, 4:8]]
     defect = up(f0[0, 0, 0, 4:8] - (26.0 * c[0] - around0(s, c, 0)))
     for i in range(4):
         dcb[pl.ds(i, 8, stride=4), :] = defect[i]
-    for k, (dz, dy) in enumerate(halo):
-        z_from, count, z_to = field_rows[dz]
-        copy = remote(
-            own.at[:, pl.ds(8 * z_from, 8 * count), :],
-            fw.at[1 - dy, :, pl.ds(8 * z_to, 8 * count), :],
-            fs.at[k], fr.at[k], at(dz, dy),
-        )
-        copy.start()
-        field_copies.append(copy)
+    for zp in range(2):
+        for yp in range(2):
+            for xp in range(2):
+                for i in range(4, 8):
+                    own[xp, window(zp, yp, i)[1], :] = v0[zp, yp, xp, i]
     coarse_copies = []
     for k, (slot, dz, dy) in enumerate(coarse_sends):
         first, count = (8, 8) if slot == 0 else (0, 16)
@@ -228,21 +228,8 @@
         )
         copy.start()
         coarse_copies.append(copy)
+    field_copies = border(own, fw, {0: (3, 8, 3), 1: (8, 3, 0), -1: (3, 4, 11)}, fs, fr)
     dall[gy, 32:48, :] = dcb[0:16, :]
-
-    for copy in field_copies:
-        copy.wait_recv()
-    for zp in range(2):
-        for yp in range(2):
-            for xp in range(2):
-                for i in range(12):
-                    yb, rows = window(zp, yp, i)
-                    value = fw[yb, xp, rows, :] * mk[zp, i]
-                    if yb == 1:
-                        value = jnp.where(own_rows(zp, (8, 128)), v0[zp, yp, xp, i], value)
-                    v0[zp, yp, xp, i] = value
-                    if zp == 1:
-                        p0[zp, yp, xp, i] = pair0(zp, value)
 
     for copy in coarse_copies:
         copy.wait_recv()
@@ -317,6 +304,19 @@
     for i in range(4):
         for zp in range(2):
             vc[i, pl.ds(zp, 8, stride=2), :] = v1[zp, i % 2, 1 + 2 * gy + i // 2]
+    for copy in field_copies:
+        copy.wait_recv()
+    for zp in range(2):
+        for yp in range(2):
+            for xp in range(2):
+                for i in range(12):
+                    yb, rows = window(zp, yp, i)
+                    value = fw[yb, xp, rows, :] * mk[zp, i]
+                    if yb == 1:
+                        value = jnp.where(own_rows(zp, (8, 128)), v0[zp, yp, xp, i], value)
+                    v0[zp, yp, xp, i] = value
+                    if zp == 1:
+                        p0[zp, yp, xp, i] = pair0(zp, value)
     for i in range(4):
         v0[0, 0, 0, 4 + i] += jnp.where(own_rows(0, (8, 128)), vc[i, 7:15, :], 0.0)
 
@@ -359,6 +359,12 @@
     for t, target in enumerate((prec, imag)):
         block = jnp.concatenate([stage[t, 0, 24:88, :], stage[t, 1, 24:88, :]], axis=1)
         target[...] = permuted(block, merge).reshape(8, 8, 256)
+    out_copies = [
+        pltpu.make_async_copy(prec, prec_hbm, io.at[1]),
+        pltpu.make_async_copy(imag, imag_hbm, io.at[2]),
+    ]
+    for copy in out_copies:
+        copy.start()
 
     for copy in first_copies:
         copy.wait_recv()
@@ -375,10 +381,9 @@
     left = lanes((1, 128)) < 64
     total_n = jnp.sum(jnp.where(left, part, 0.0), axis=1, keepdims=True)
     total_d = jnp.sum(jnp.where(left, 0.0, part), axis=1, keepdims=True)
-    alpha = (total_n / total_d)[:, :, None]
-    sol_ref[...] = alpha * prec[...]
-    res_ref[...] = r_ref[...] - alpha * imag[...]
-
+    alpha_ref[...] = total_n / total_d
+    for copy in out_copies:
+        copy.wait()
     for copy in rhs_copies + field_copies + coarse_copies + first_copies + second_copies:
         copy.wait_send()
 
@@ -394,14 +399,19 @@
         out = jax.ShapeDtypeStruct(right_side.shape, F32)
         vm = pltpu.VMEM
         dma = pltpu.SemaphoreType.DMA
-        return pl.pallas_call(
+        precond, image, alpha = pl.pallas_call(
             functools.partial(kernel, ngz, ngy),
             name="cg_iteration",
-            out_shape=(out, out),
-            in_specs=[pl.BlockSpec(memory_space=pltpu.VMEM)],
-            out_specs=(pl.BlockSpec(memory_space=pltpu.VMEM), pl.BlockSpec(memory_space=pltpu.VMEM)),
+            out_shape=(out, out, jax.ShapeDtypeStruct((1, 1), F32)),
+            in_specs=[pl.BlockSpec(memory_space=pl.ANY)],
+            out_specs=(
+                pl.BlockSpec(memory_space=pl.ANY),
+                pl.BlockSpec(memory_space=pl.ANY),
+                pl.BlockSpec(memory_space=pltpu.VMEM),
+            ),
             scratch_shapes=[
-                vm((3, 16, 8, 256), F32),
+                vm((8, 8, 256), F32),
+                vm((2, 64, 128), F32),
                 vm((3, 2, 128, 128), F32),
                 vm((2, 2, 2, 12, 8, 128), F32),
                 vm((2, 2, 2, 12, 8, 128), F32),
@@ -423,11 +433,12 @@
                 vm((2, 1, 128), F32),
                 vm((one, 1, 128), F32),
                 vm((two, 1, 128), F32),
-                dma((8,)), dma((8,)), dma((8,)), dma((8,)), dma((coarse,)), dma((coarse,)),
+                dma((3,)), dma((8,)), dma((8,)), dma((8,)), dma((8,)), dma((coarse,)), dma((coarse,)),
                 dma((one,)), dma((one,)), dma((two,)), dma((two,)),
             ],
             compiler_params=pltpu.CompilerParams(collective_id=0, has_side_effects=True),
         )(right_side)
+        return alpha[:, :, None] * precond, right_side - alpha[:, :, None] * image
 
     return jax.shard_map(
         body,

time: 59 us -> 55.2 us (0.936)
  Pallas kernels: 56 us -> 52.2 us
  other arithmetic: 0 us -> 2.17 us
  local copies, waits for them, and re-layouts: 2.14 us -> 0.01 us
    pallas_call x1, Pallas kernels: 56 us -> 52.2 us  [body(): pl.pallas_call(functools.partial(kernel, ngz, ngy), name='cg_iteration',...]
    sub x0 -> x1, other arithmetic: none -> 2.17 us  [body(): return (alpha[:, :, None] * precond, right_side - alpha[:, :, None] * image)]
    unnamed x4 -> x2, local copies, waits for them, and re-layouts: 2.14 us -> 0.01 us
where the time goes in v2:
time: 55.2 us; the launch traced here: 55 us
  Pallas kernels  52.2 us (95%)
  other arithmetic  2.17 us (4%)
  between operations  0.65 us (1%)
    pallas_call x1, Pallas kernels, body(): pl.pallas_call(functools.partial(kernel, ngz, ngy), name='cg_iteration',...  52.2 us
    sub x1, other arithmetic, body(): return (alpha[:, :, None] * precond, right_side - alpha[:, :, None] * image)  2.17 us

profile of v2, /device:TPU:1, one launch (start us, length us, event | category | flops | bytes accessed | tf_op | source)
XLA Modules:
  0.0 55.0 jit_solution(10934192951467841458)
XLA Ops:
  0.6 0.0 copy-start
  0.6 52.2 %cg_iteration.1 = (f32[8,8,256]{2,1,0:T(8,128)}, f32[8,8,256]{2,1,0:T(8,128)}, f32[1,1]{1,0:T(1,128)}) custom-call(f32[8,8,256]{2,1,0:T(8,128)} %r_hbm.1), custom_call_target="tpu_custom_call" | custom-call | tf_op jit(solution)/shard_map/cg_iteration/pallas_call | solution.py:402
  52.8 0.0 copy-done
  52.9 2.2 %multiply_subtract_fusion = (f32[8,8,256]{2,1,0:T(8,128)}, f32[8,8,256]{2,1,0:T(8,128)}) fusion(f32[8,8,256]{2,1,0:T(8,128)S(1)} %copy-done, f32[8,8,256]{2,1,0:T(8,128)} %get-tuple-element.7, f32[]{:T(128)} %bitcast, f32[8,8,256]{2,1,0:T(8,128)} %get-tuple-element.6), kind=kLoop, calls=%fused_computation | loop fusion | flops 49152 | bytes 327684 | tf_op jit(solution)/shard_map/sub | solution.py:441
Async XLA Ops:
  0.6 52.2 %copy-start = (f32[8,8,256]{2,1,0:T(8,128)S(1)}, f32[8,8,256]{2,1,0:T(8,128)}, u32[]{:S(2)}) copy-start(f32[8,8,256]{2,1,0:T(8,128)} %r_hbm.1) | copy-start | bytes 196612

commit v3 on v2

--- a/solution.py
+++ b/solution.py
@@ -64,7 +64,7 @@
 def kernel(
     ngz, ngy, r_hbm, prec_hbm, imag_hbm, alpha_ref,
     rin, ownr, rd, f0, v0, p0, mk, own, fw, dcb, dall, f1, v1, p1, f2, v2, vc, stage, prec, imag, sb, ar1, ar2,
-    io, rs, rr, fs, fr, cs, cr, s1, r1, s2, r2,
+    near, far, beside, io, rs, rr, fs, fr, cs, cr, s1, r1, s2, r2,
 ):
     gz = lax.axis_index("gz")
     gy = lax.axis_index("gy")
@@ -100,29 +100,43 @@
     load.start()
 
     barrier = pltpu.get_barrier_semaphore()
-    for c, z in first_group:
-        pl.semaphore_signal(barrier, inc=1, device_id=along_z(-c, -z), device_id_type=MESH)
-    for x, y in second_group:
-        pl.semaphore_signal(barrier, inc=1, device_id=along_xy(-x, -y), device_id_type=MESH)
-    for slot, dz, dy in coarse_sends:
+    for dz, dy in halo:
         pl.semaphore_signal(barrier, inc=1, device_id=at(-dz, -dy), device_id_type=MESH)
+
+    def tell(semaphore, offsets):
+        for dz, dy in offsets:
+            pl.semaphore_signal(semaphore, inc=1, device_id=at(dz, dy), device_id_type=MESH)
+
+    reach = 4
+    rounds = []
+    while reach < ngz // 2 + 1:
+        rounds.append([(reach, 0), (-reach, 0)])
+        reach *= 2
+    done = []
+
+    def advance():
+        k = len(done)
+        if 0 < k <= len(rounds):
+            pl.semaphore_wait(far.at[k - 1], 2)
+        if k < len(rounds):
+            tell(far.at[k], rounds[k])
+        done.append(k)
 
     row = lax.broadcasted_iota(jnp.int32, (256, 256), 0)
     col = lax.broadcasted_iota(jnp.int32, (256, 256), 1)
-    split = (row == jnp.where(col < 128, 2 * col, 2 * col - 255)).astype(F32)
-    merge = (col == jnp.where(row < 128, 2 * row, 2 * row - 255)).astype(F32)
+    split = (row == jnp.where(col < 128, 2 * col, 2 * col - 255)).astype(F32).astype(jnp.bfloat16)
+    merge = (col == jnp.where(row < 128, 2 * row, 2 * row - 255)).astype(F32).astype(jnp.bfloat16)
 
     def permuted(block, matrix):
-        return lax.dot_general(
-            block, matrix, (((1,), (0,)), ((), ())), precision=lax.Precision.HIGHEST, preferred_element_type=F32
-        )
-
-    load.wait()
-    both = permuted(rin[...].reshape(64, 256), split)
-    for xp in range(2):
-        part = both[:, 128 * xp : 128 * xp + 128]
-        ownr[xp] = part
-        rd[1, xp, 24:88, :] = part
+        high = block.astype(jnp.bfloat16)
+        rest = block - high.astype(F32)
+        middle = rest.astype(jnp.bfloat16)
+        low = (rest - middle.astype(F32)).astype(jnp.bfloat16)
+        moved = [
+            lax.dot_general(part, matrix, (((1,), (0,)), ((), ())), preferred_element_type=F32)
+            for part in (high, middle, low)
+        ]
+        return (moved[0] + moved[1]) + moved[2]
 
     for yb in range(3):
         rd[yb, :, 0:8, :] = jnp.zeros((2, 8, 128), F32)
@@ -136,6 +150,13 @@
     p1[...] = jnp.zeros(p1.shape, F32)
     v2[...] = jnp.zeros(v2.shape, F32)
 
+    load.wait()
+    both = permuted(rin[...].reshape(64, 256), split)
+    for xp in range(2):
+        part = both[:, 128 * xp : 128 * xp + 128]
+        ownr[xp] = part
+        rd[1, xp, 24:88, :] = part
+
     sub = sublanes((8, 128))
     for zp in range(2):
         z = gz * 8 + 2 * sub - (2 + zp)
@@ -150,7 +171,7 @@
         s = sublanes(shape)
         return (s >= 1 + zp) & (s < 5 + zp)
 
-    pl.semaphore_wait(barrier, len(coarse_sends) + len(first_group) + len(second_group))
+    pl.semaphore_wait(barrier, len(halo))
 
     def border(source, target, rows, sends, arrivals):
         copies = []
@@ -168,6 +189,7 @@
     rhs_copies = border(ownr, rd, {0: (0, 8, 3), 1: (6, 2, 1), -1: (0, 3, 11)}, rs, rr)
     for copy in rhs_copies:
         copy.wait_recv()
+    tell(near, [(0, 2), (0, -2), (2, 0), (-2, 0)])
 
     def window(zp, yp, i):
         return i // 4, pl.ds(8 * (1 - zp) + 2 * (i % 4) + yp, 8, stride=16)
@@ -219,6 +241,7 @@
             for xp in range(2):
                 for i in range(4, 8):
                     own[xp, window(zp, yp, i)[1], :] = v0[zp, yp, xp, i]
+    pl.semaphore_wait(near, 4)
     coarse_copies = []
     for k, (slot, dz, dy) in enumerate(coarse_sends):
         first, count = (8, 8) if slot == 0 else (0, 16)
@@ -231,8 +254,11 @@
     field_copies = border(own, fw, {0: (3, 8, 3), 1: (8, 3, 0), -1: (3, 4, 11)}, fs, fr)
     dall[gy, 32:48, :] = dcb[0:16, :]
 
+    for _ in range(3):
+        advance()
     for copy in coarse_copies:
         copy.wait_recv()
+    tell(beside, [(-1, 0)])
 
     n1 = 2 * ngy
     for zp in range(2):
@@ -267,6 +293,7 @@
 
     for group, order in SWEEP:
         phase1(group, order)
+    advance()
 
     n2 = ngy
     s = outer1(0, 0)
@@ -300,6 +327,10 @@
         p1[0, 0, 1 + i] = pair1(0, value)
     for group, order in SWEEP:
         phase1(group, order)
+
+    while len(done) <= len(rounds):
+        advance()
+    pl.semaphore_wait(beside, 1)
 
     for i in range(4):
         for zp in range(2):
@@ -402,8 +433,8 @@
         precond, image, alpha = pl.pallas_call(
             functools.partial(kernel, ngz, ngy),
             name="cg_iteration",
-            out_shape=(out, out, jax.ShapeDtypeStruct((1, 1), F32)),
-            in_specs=[pl.BlockSpec(memory_space=pl.ANY)],
+            out_shape=(pltpu.VMEM(right_side.shape, F32), pltpu.VMEM(right_side.shape, F32), jax.ShapeDtypeStruct((1, 1), F32)),
+            in_specs=[pl.BlockSpec(memory_space=pltpu.HBM)],
             out_specs=(
                 pl.BlockSpec(memory_space=pl.ANY),
                 pl.BlockSpec(memory_space=pl.ANY),
@@ -433,10 +464,11 @@
                 vm((2, 1, 128), F32),
                 vm((one, 1, 128), F32),
                 vm((two, 1, 128), F32),
+                pltpu.SemaphoreType.REGULAR, pltpu.SemaphoreType.REGULAR((8,)), pltpu.SemaphoreType.REGULAR,
                 dma((3,)), dma((8,)), dma((8,)), dma((8,)), dma((8,)), dma((coarse,)), dma((coarse,)),
                 dma((one,)), dma((one,)), dma((two,)), dma((two,)),
             ],
-            compiler_params=pltpu.CompilerParams(collective_id=0, has_side_effects=True),
+            compiler_params=pltpu.CompilerParams(collective_id=0, has_side_effects=True, vmem_limit_bytes=60000000),
         )(right_side)
         return alpha[:, :, None] * precond, right_side - alpha[:, :, None] * image
 

time: 55.2 us -> 54.8 us (level)
  other arithmetic: 2.17 us -> 1.3 us
    sub x1, other arithmetic: 2.17 us -> 1.3 us  [body(): return (alpha[:, :, None] * precond, right_side - alpha[:, :, None] * image)]
where the time goes in v3:
time: 54.8 us; the launch traced here: 54.6 us
  Pallas kernels  52.6 us (96%)
  other arithmetic  1.3 us (2%)
  between operations  0.65 us (1%)
    pallas_call x1, Pallas kernels, body(): pl.pallas_call(functools.partial(kernel, ngz, ngy), name='cg_iteration',...  52.6 us
    sub x1, other arithmetic, body(): return (alpha[:, :, None] * precond, right_side - alpha[:, :, None] * image)  1.3 us

profile of v3, /device:TPU:1, one launch (start us, length us, event | category | flops | bytes accessed | tf_op | source)
XLA Modules:
  0.0 54.6 jit_solution(4341623493344741644)
XLA Ops:
  0.6 0.0 copy-start
  0.6 52.6 %cg_iteration.1 = (f32[8,8,256]{2,1,0:T(8,128)S(1)}, f32[8,8,256]{2,1,0:T(8,128)S(1)}, f32[1,1]{1,0:T(1,128)}) custom-call(f32[8,8,256]{2,1,0:T(8,128)} %r_hbm.1), custom_call_target="tpu_custom_call" | custom-call | tf_op jit(solution)/shard_map/cg_iteration/pallas_call | solution.py:433
  53.3 0.0 copy-done
  53.3 1.3 %multiply_subtract_fusion = (f32[8,8,256]{2,1,0:T(8,128)}, f32[8,8,256]{2,1,0:T(8,128)}) fusion(f32[8,8,256]{2,1,0:T(8,128)S(1)} %copy-done, f32[8,8,256]{2,1,0:T(8,128)S(1)} %get-tuple-element.7, f32[]{:T(128)} %bitcast, f32[8,8,256]{2,1,0:T(8,128)S(1)} %get-tuple-element.6), kind=kLoop, calls=%fused_computation | loop fusion | flops 49152 | bytes 327684 | tf_op jit(solution)/shard_map/sub | solution.py:473
Async XLA Ops:
  0.6 52.7 %copy-start = (f32[8,8,256]{2,1,0:T(8,128)S(1)}, f32[8,8,256]{2,1,0:T(8,128)}, u32[]{:S(2)}) copy-start(f32[8,8,256]{2,1,0:T(8,128)} %r_hbm.1) | copy-start | bytes 196612

commit v4 on v3

--- a/solution.py
+++ b/solution.py
@@ -86,7 +86,7 @@
 
     coarse_sends = [
         (slot, dz, dy)
-        for dy in sorted(range(ngy), key=lambda d: -min(d, ngy - d))
+        for dy in sorted(range(ngy), key=lambda d: (min(d, ngy - d) > 2, -min(d, ngy - d)))
         for slot, dz in ((2, 0), (1, 1), (3, -1), (0, 2))
         if not (dz == 0 and dy == 0)
     ]
@@ -100,27 +100,17 @@
     load.start()
 
     barrier = pltpu.get_barrier_semaphore()
-    for dz, dy in halo:
-        pl.semaphore_signal(barrier, inc=1, device_id=at(-dz, -dy), device_id_type=MESH)
-
-    def tell(semaphore, offsets):
-        for dz, dy in offsets:
-            pl.semaphore_signal(semaphore, inc=1, device_id=at(dz, dy), device_id_type=MESH)
-
-    reach = 4
-    rounds = []
-    while reach < ngz // 2 + 1:
-        rounds.append([(reach, 0), (-reach, 0)])
-        reach *= 2
-    done = []
-
-    def advance():
-        k = len(done)
-        if 0 < k <= len(rounds):
-            pl.semaphore_wait(far.at[k - 1], 2)
-        if k < len(rounds):
-            tell(far.at[k], rounds[k])
-        done.append(k)
+    greeted = [at(dz, dy) for dz, dy in halo]
+    greeted += [along_z(0, z) for z in (1, -1, 2, -2) if z % nz]
+    greeted += [along_xy(x, 0) for x in range(1, NX_CHIPS)]
+
+    def tell(semaphore, devices):
+        for device in devices:
+            pl.semaphore_signal(semaphore, inc=1, device_id=device, device_id_type=MESH)
+
+    tell(barrier, greeted)
+    two_away = [along_z(0, z) for z in (2, -2) if z % nz]
+    three_away = [along_z(0, z) for z in (3, -3) if z % nz]
 
     row = lax.broadcasted_iota(jnp.int32, (256, 256), 0)
     col = lax.broadcasted_iota(jnp.int32, (256, 256), 1)
@@ -171,7 +161,7 @@
         s = sublanes(shape)
         return (s >= 1 + zp) & (s < 5 + zp)
 
-    pl.semaphore_wait(barrier, len(halo))
+    pl.semaphore_wait(barrier, len(greeted))
 
     def border(source, target, rows, sends, arrivals):
         copies = []
@@ -186,10 +176,14 @@
             copies.append(copy)
         return copies
 
+    tell(far.at[0], two_away)
     rhs_copies = border(ownr, rd, {0: (0, 8, 3), 1: (6, 2, 1), -1: (0, 3, 11)}, rs, rr)
     for copy in rhs_copies:
         copy.wait_recv()
-    tell(near, [(0, 2), (0, -2), (2, 0), (-2, 0)])
+    tell(near, [at(0, 2), at(0, -2)])
+    if two_away:
+        pl.semaphore_wait(far.at[0], len(two_away))
+    tell(far.at[1], three_away)
 
     def window(zp, yp, i):
         return i // 4, pl.ds(8 * (1 - zp) + 2 * (i % 4) + yp, 8, stride=16)
@@ -241,9 +235,11 @@
             for xp in range(2):
                 for i in range(4, 8):
                     own[xp, window(zp, yp, i)[1], :] = v0[zp, yp, xp, i]
-    pl.semaphore_wait(near, 4)
     coarse_copies = []
+    reached = sum(min(dy, ngy - dy) <= 2 for _, _, dy in coarse_sends) % len(coarse_sends)
     for k, (slot, dz, dy) in enumerate(coarse_sends):
+        if k == reached:
+            pl.semaphore_wait(near, 2)
         first, count = (8, 8) if slot == 0 else (0, 16)
         copy = remote(
             dcb.at[pl.ds(first, count), :], dall.at[gy, pl.ds(16 * slot + first, count), :],
@@ -254,11 +250,11 @@
     field_copies = border(own, fw, {0: (3, 8, 3), 1: (8, 3, 0), -1: (3, 4, 11)}, fs, fr)
     dall[gy, 32:48, :] = dcb[0:16, :]
 
-    for _ in range(3):
-        advance()
     for copy in coarse_copies:
         copy.wait_recv()
-    tell(beside, [(-1, 0)])
+    if three_away:
+        pl.semaphore_wait(far.at[1], len(three_away))
+    tell(beside, [along_z(1, 0)])
 
     n1 = 2 * ngy
     for zp in range(2):
@@ -293,7 +289,6 @@
 
     for group, order in SWEEP:
         phase1(group, order)
-    advance()
 
     n2 = ngy
     s = outer1(0, 0)
@@ -328,8 +323,6 @@
     for group, order in SWEEP:
         phase1(group, order)
 
-    while len(done) <= len(rounds):
-        advance()
     pl.semaphore_wait(beside, 1)
 
     for i in range(4):
@@ -464,7 +457,7 @@
                 vm((2, 1, 128), F32),
                 vm((one, 1, 128), F32),
                 vm((two, 1, 128), F32),
-                pltpu.SemaphoreType.REGULAR, pltpu.SemaphoreType.REGULAR((8,)), pltpu.SemaphoreType.REGULAR,
+                pltpu.SemaphoreType.REGULAR, pltpu.SemaphoreType.REGULAR((2,)), pltpu.SemaphoreType.REGULAR,
                 dma((3,)), dma((8,)), dma((8,)), dma((8,)), dma((8,)), dma((coarse,)), dma((coarse,)),
                 dma((one,)), dma((one,)), dma((two,)), dma((two,)),
             ],

time: 54.8 us -> 52.3 us (0.954)
  Pallas kernels: 52.6 us -> 50.1 us
    pallas_call x1, Pallas kernels: 52.6 us -> 50.1 us  [body(): pl.pallas_call(functools.partial(kernel, ngz, ngy), name='cg_iteration',...]
where the time goes in v4:
time: 52.3 us; the launch traced here: 52.1 us
  Pallas kernels  50.1 us (96%)
  other arithmetic  1.3 us (2%)
  between operations  0.65 us (1%)
    pallas_call x1, Pallas kernels, body(): pl.pallas_call(functools.partial(kernel, ngz, ngy), name='cg_iteration',...  50.1 us
    sub x1, other arithmetic, body(): return (alpha[:, :, None] * precond, right_side - alpha[:, :, None] * image)  1.3 us

profile of v4, /device:TPU:1, one launch (start us, length us, event | category | flops | bytes accessed | tf_op | source)
XLA Modules:
  0.0 52.1 jit_solution(8046324248685304376)
XLA Ops:
  0.6 0.0 copy-start
  0.6 50.1 %cg_iteration.1 = (f32[8,8,256]{2,1,0:T(8,128)S(1)}, f32[8,8,256]{2,1,0:T(8,128)S(1)}, f32[1,1]{1,0:T(1,128)}) custom-call(f32[8,8,256]{2,1,0:T(8,128)} %r_hbm.1), custom_call_target="tpu_custom_call" | custom-call | tf_op jit(solution)/shard_map/cg_iteration/pallas_call | solution.py:426
  50.8 0.0 copy-done
  50.8 1.3 %multiply_subtract_fusion = (f32[8,8,256]{2,1,0:T(8,128)}, f32[8,8,256]{2,1,0:T(8,128)}) fusion(f32[8,8,256]{2,1,0:T(8,128)S(1)} %copy-done, f32[8,8,256]{2,1,0:T(8,128)S(1)} %get-tuple-element.7, f32[]{:T(128)} %bitcast, f32[8,8,256]{2,1,0:T(8,128)S(1)} %get-tuple-element.6), kind=kLoop, calls=%fused_computation | loop fusion | flops 49152 | bytes 327684 | tf_op jit(solution)/shard_map/sub | solution.py:466
Async XLA Ops:
  0.6 50.2 %copy-start = (f32[8,8,256]{2,1,0:T(8,128)S(1)}, f32[8,8,256]{2,1,0:T(8,128)}, u32[]{:S(2)}) copy-start(f32[8,8,256]{2,1,0:T(8,128)} %r_hbm.1) | copy-start | bytes 196612

commit v5 on v4

--- a/solution.py
+++ b/solution.py
@@ -46,6 +46,15 @@
     return from_left(u, step) + from_right(u, step)
 
 
+def two_colours(base, f_sides, u, scale, step):
+    sides = both_sides(u, step)
+    place = lanes(u.shape)
+    own = jnp.where(place >= step, u, 0.0) + jnp.where(place < 128 - step, u, 0.0)
+    twice = both_sides(u, 2 * step) + own
+    first = base + sides
+    return first * scale, (first + (sides + f_sides + twice) * scale) * scale
+
+
 def down(u):
     return pltpu.roll(u, 1, u.ndim - 2)
 
@@ -63,7 +72,7 @@
 
 def kernel(
     ngz, ngy, r_hbm, prec_hbm, imag_hbm, alpha_ref,
-    rin, ownr, rd, f0, v0, p0, mk, own, fw, dcb, dall, f1, v1, p1, f2, v2, vc, stage, prec, imag, sb, ar1, ar2,
+    rin, ownr, rd, g0, g1, g2, f0, v0, p0, mk, own, fw, dcb, dall, f1, v1, p1, f2, v2, vc, stage, prec, imag, sb, ar1, ar2,
     near, far, beside, io, rs, rr, fs, fr, cs, cr, s1, r1, s2, r2,
 ):
     gz = lax.axis_index("gz")
@@ -193,7 +202,9 @@
             for xp in range(2):
                 for i in range(12):
                     yb, rows = window(zp, yp, i)
-                    f0[zp, yp, xp, i] = rd[yb, xp, rows, :]
+                    value = rd[yb, xp, rows, :]
+                    f0[zp, yp, xp, i] = value
+                    g0[zp, yp, xp, i] = value + (from_right(value) if xp == 0 else from_left(value))
 
     def pair0(zp, c):
         return c + (down(c) if zp == 0 else up(c))
@@ -207,17 +218,28 @@
             sums.append(s + q + p0[1 - zp, yp, xp, lo:hi])
         return sums
 
+    def beside0(u, xp):
+        return u + (from_left(u) if xp == 0 else from_right(u))
+
     def around0(s, c, xp):
-        other = s[1 - xp] + c[1 - xp]
-        return s[xp] + (other + (from_left(other) if xp == 0 else from_right(other)))
+        return s[xp] + beside0(s[1 - xp] + c[1 - xp], xp)
 
     def phase0(group, order, lo, hi):
         zp, yp = group
         s = outer0(zp, yp, lo, hi)
         c = [v0[zp, yp, 0, lo:hi], v0[zp, yp, 1, lo:hi]]
         scale = mk[zp, lo:hi] * INV
-        for xp in order:
-            c[xp] = (around0(s, c, xp) + f0[zp, yp, xp, lo:hi]) * scale
+        f = [f0[zp, yp, 0, lo:hi], f0[zp, yp, 1, lo:hi]]
+        a, b = order[:2]
+        u = s[b] + c[b]
+        left, right = from_left(u), from_right(u)
+        edge = lanes(u.shape) < 127 if a == 0 else lanes(u.shape) >= 1
+        twice = u + left + right + jnp.where(edge, u, 0.0)
+        cross = beside0(s[a], b)
+        c[a] = (s[a] + f[a] + (u + (left if a == 0 else right))) * scale
+        c[b] = (s[b] + f[b] + cross + (cross + g0[zp, yp, a, lo:hi] + twice) * scale) * scale
+        for xp in order[2:]:
+            c[xp] = (around0(s, c, xp) + f[xp]) * scale
         for xp in range(2):
             v0[zp, yp, xp, lo:hi] = c[xp]
             p0[zp, yp, xp, lo:hi] = pair0(zp, c[xp])
@@ -260,7 +282,9 @@
     for zp in range(2):
         for yp in range(2):
             for i in range(n1):
-                f1[zp, yp, i] = dall[i // 2, pl.ds(2 * (i % 2) + yp + 4 * zp, 8, stride=8), :]
+                value = dall[i // 2, pl.ds(2 * (i % 2) + yp + 4 * zp, 8, stride=8), :]
+                f1[zp, yp, i] = value
+                g1[zp, yp, i] = both_sides(value)
 
     scale1 = []
     for zp in range(2):
@@ -282,7 +306,10 @@
         c = v1[zp, yp, 1 : 1 + n1]
         base = s + f1[zp, yp]
         parity = lax.rem(lanes(c.shape), 2)
-        for xp in order:
+        u = s + jnp.where(parity == order[1], c, 0.0)
+        first, second = two_colours(base, g1[zp, yp], u, scale1[zp], 1)
+        c = jnp.where(parity == order[0], first, second)
+        for xp in order[2:]:
             c = jnp.where(parity == xp, (base + both_sides(s + c)) * scale1[zp], c)
         v1[zp, yp, 1 : 1 + n1] = c
         p1[zp, yp, 1 : 1 + n1] = pair1(zp, c)
@@ -297,6 +324,7 @@
     defect = jnp.where(even, f1[0, 0] - (26.0 * c - (s + both_sides(s + c))), 0.0)
     for i in range(n1):
         f2[i % 2, i // 2] = defect[i]
+        g2[i % 2, i // 2] = both_sides(defect[i], 2)
     z = gz * 2 + sub - 4
     scale2 = jnp.where((z >= 0) & (z < ngz * 2), INV, 0.0).astype(F32)[None]
 
@@ -310,7 +338,10 @@
         base = s + f2[yp]
         layer = lax.rem(sublanes(c.shape), 2) == zp
         place = lax.rem(lanes(c.shape), 4)
-        for xp in order:
+        u = s + jnp.where(place == 2 * order[1], c, 0.0)
+        first, second = two_colours(base, g2[yp], u, scale2, 2)
+        c = jnp.where(layer & (place == 2 * order[0]), first, jnp.where(layer & (place == 2 * order[1]), second, c))
+        for xp in order[2:]:
             c = jnp.where(layer & (place == 2 * xp), (base + both_sides(s + c, 2)) * scale2, c)
         v2[yp, 1 : 1 + n2] = c
 
@@ -437,6 +468,9 @@
                 vm((8, 8, 256), F32),
                 vm((2, 64, 128), F32),
                 vm((3, 2, 128, 128), F32),
+                vm((2, 2, 2, 12, 8, 128), F32),
+                vm((2, 2, 2 * ngy, 8, 128), F32),
+                vm((2, ngy, 8, 128), F32),
                 vm((2, 2, 2, 12, 8, 128), F32),
                 vm((2, 2, 2, 12, 8, 128), F32),
                 vm((2, 2, 2, 12, 8, 128), F32),

time: 52.3 us -> 50.7 us (0.969)
  Pallas kernels: 50.1 us -> 48.6 us
    pallas_call x1, Pallas kernels: 50.1 us -> 48.6 us  [body(): pl.pallas_call(functools.partial(kernel, ngz, ngy), name='cg_iteration',...]
where the time goes in v5:
time: 50.7 us; the launch traced here: 50.5 us
  Pallas kernels  48.6 us (96%)
  other arithmetic  1.3 us (3%)
  between operations  0.65 us (1%)
    pallas_call x1, Pallas kernels, body(): pl.pallas_call(functools.partial(kernel, ngz, ngy), name='cg_iteration',...  48.6 us
    sub x1, other arithmetic, body(): return (alpha[:, :, None] * precond, right_side - alpha[:, :, None] * image)  1.3 us

profile of v5, /device:TPU:1, one launch (start us, length us, event | category | flops | bytes accessed | tf_op | source)
XLA Modules:
  0.0 50.5 jit_solution(15552929386901869457)
XLA Ops:
  0.6 0.0 copy-start
  0.6 48.6 %cg_iteration.1 = (f32[8,8,256]{2,1,0:T(8,128)S(1)}, f32[8,8,256]{2,1,0:T(8,128)S(1)}, f32[1,1]{1,0:T(1,128)}) custom-call(f32[8,8,256]{2,1,0:T(8,128)} %r_hbm.1), custom_call_target="tpu_custom_call" | custom-call | tf_op jit(solution)/shard_map/cg_iteration/pallas_call | solution.py:457
  49.2 0.0 copy-done
  49.2 1.3 %multiply_subtract_fusion = (f32[8,8,256]{2,1,0:T(8,128)}, f32[8,8,256]{2,1,0:T(8,128)}) fusion(f32[8,8,256]{2,1,0:T(8,128)S(1)} %copy-done, f32[8,8,256]{2,1,0:T(8,128)S(1)} %get-tuple-element.7, f32[]{:T(128)} %bitcast, f32[8,8,256]{2,1,0:T(8,128)S(1)} %get-tuple-element.6), kind=kLoop, calls=%fused_computation | loop fusion | flops 49152 | bytes 327684 | tf_op jit(solution)/shard_map/sub | solution.py:500
Async XLA Ops:
  0.6 48.6 %copy-start = (f32[8,8,256]{2,1,0:T(8,128)S(1)}, f32[8,8,256]{2,1,0:T(8,128)}, u32[]{:S(2)}) copy-start(f32[8,8,256]{2,1,0:T(8,128)} %r_hbm.1) | copy-start | bytes 196612

commit v6 on v5

--- a/solution.py
+++ b/solution.py
@@ -345,20 +345,6 @@
             c = jnp.where(layer & (place == 2 * xp), (base + both_sides(s + c, 2)) * scale2, c)
         v2[yp, 1 : 1 + n2] = c
 
-    held = sublanes((8, 128))
-    mine = (held >= 4) & (held < 6)
-    for i in range(n1):
-        value = v1[0, 0, 1 + i] + jnp.where(mine, v2[i % 2, 1 + i // 2], 0.0)
-        v1[0, 0, 1 + i] = value
-        p1[0, 0, 1 + i] = pair1(0, value)
-    for group, order in SWEEP:
-        phase1(group, order)
-
-    pl.semaphore_wait(beside, 1)
-
-    for i in range(4):
-        for zp in range(2):
-            vc[i, pl.ds(zp, 8, stride=2), :] = v1[zp, i % 2, 1 + 2 * gy + i // 2]
     for copy in field_copies:
         copy.wait_recv()
     for zp in range(2):
@@ -372,6 +358,21 @@
                     v0[zp, yp, xp, i] = value
                     if zp == 1:
                         p0[zp, yp, xp, i] = pair0(zp, value)
+
+    held = sublanes((8, 128))
+    mine = (held >= 4) & (held < 6)
+    for i in range(n1):
+        value = v1[0, 0, 1 + i] + jnp.where(mine, v2[i % 2, 1 + i // 2], 0.0)
+        v1[0, 0, 1 + i] = value
+        p1[0, 0, 1 + i] = pair1(0, value)
+    for group, order in SWEEP:
+        phase1(group, order)
+
+    pl.semaphore_wait(beside, 1)
+
+    for i in range(4):
+        for zp in range(2):
+            vc[i, pl.ds(zp, 8, stride=2), :] = v1[zp, i % 2, 1 + 2 * gy + i // 2]
     for i in range(4):
         v0[0, 0, 0, 4 + i] += jnp.where(own_rows(0, (8, 128)), vc[i, 7:15, :], 0.0)
 

time: 50.7 us -> 51 us (level)
  no operation moved by 1% of the time
where the time goes in v6:
time: 51 us; the launch traced here: 50.8 us
  Pallas kernels  48.8 us (96%)
  other arithmetic  1.3 us (3%)
  between operations  0.65 us (1%)
    pallas_call x1, Pallas kernels, body(): pl.pallas_call(functools.partial(kernel, ngz, ngy), name='cg_iteration',...  48.8 us
    sub x1, other arithmetic, body(): return (alpha[:, :, None] * precond, right_side - alpha[:, :, None] * image)  1.3 us

profile of v6, /device:TPU:1, one launch (start us, length us, event | category | flops | bytes accessed | tf_op | source)
XLA Modules:
  0.0 50.8 jit_solution(13644059634171761567)
XLA Ops:
  0.6 0.0 copy-start
  0.6 48.8 %cg_iteration.1 = (f32[8,8,256]{2,1,0:T(8,128)S(1)}, f32[8,8,256]{2,1,0:T(8,128)S(1)}, f32[1,1]{1,0:T(1,128)}) custom-call(f32[8,8,256]{2,1,0:T(8,128)} %r_hbm.1), custom_call_target="tpu_custom_call" | custom-call | tf_op jit(solution)/shard_map/cg_iteration/pallas_call | solution.py:458
  49.5 0.0 copy-done
  49.5 1.3 %multiply_subtract_fusion = (f32[8,8,256]{2,1,0:T(8,128)}, f32[8,8,256]{2,1,0:T(8,128)}) fusion(f32[8,8,256]{2,1,0:T(8,128)S(1)} %copy-done, f32[8,8,256]{2,1,0:T(8,128)S(1)} %get-tuple-element.7, f32[]{:T(128)} %bitcast, f32[8,8,256]{2,1,0:T(8,128)S(1)} %get-tuple-element.6), kind=kLoop, calls=%fused_computation | loop fusion | flops 49152 | bytes 327684 | tf_op jit(solution)/shard_map/sub | solution.py:501
Async XLA Ops:
  0.6 48.8 %copy-start = (f32[8,8,256]{2,1,0:T(8,128)S(1)}, f32[8,8,256]{2,1,0:T(8,128)}, u32[]{:S(2)}) copy-start(f32[8,8,256]{2,1,0:T(8,128)} %r_hbm.1) | copy-start | bytes 196612
